TPU v7x, 32 devices: a whole 2x2x4 slice. The times are simulated.
32 devices in a mesh: grp: 8 (over z, y), col: 4 (over x, core).
Axes of the slice: x: 2, y: 2, z: 4, core: 2. Of those that a mesh axis runs over, the one named last changes fastest.
Arguments:
- features: bfloat16 [65536, 256], P(('grp', 'col')), may hold values from -6 to 6
- adj_tiles: bfloat16 [1536, 256, 256], P('grp'), may hold values from 0 to 1.5
- block_pairs: int32 [8, 192, 2], P('grp'), may hold values from 0 to 31, as said below
- tile_count: int32 [8], P('grp'), may hold values from 32 to 192, as said below
- degree: int32 [65536], P('grp'), may hold values from 1 to 769
- labels: int32 [65536], P(('grp', 'col')), may hold values from 0 to 63
- loss_mask: int32 [65536], P(('grp', 'col')), may hold values from 0 to 1
- slot_piece: int32 [8, 79], replicated, may hold values from -1 to 416, as said below
- master: float32 [632, 2, 256], P('grp', None, 'col'), may hold values from -4 to 4
- moment_one: float32 [632, 2, 256], P('grp', None, 'col'), may hold values from -0.125 to 0.125
- moment_two: float32 [632, 2, 256], P('grp', None, 'col'), may hold values from 3.0517579e-06 to 0.00030517578
Outputs:
- mean_loss: float32 [], replicated
- new_master: float32 [632, 2, 256], P('grp', None, 'col')
- new_moment_one: float32 [632, 2, 256], P('grp', None, 'col')
- new_moment_two: float32 [632, 2, 256], P('grp', None, 'col')
- new_weights: bfloat16 [632, 2, 256], P('grp', None, 'col')
Inputs may be any that keep to these rules, and one draw needn't show every extreme that they name: `block_pairs`: of each group, the first tile_count entries are distinct pairs of blocks and include every diagonal pair (r, r); later entries are padding. `tile_count`: some group has 192 live tiles in every draw. `slot_piece`: each piece 0 to 416 sits in exactly one slot; a group holds at most 79 pieces, and some group holds 79 in every draw.
All inputs are finite; a program needn't handle non-finite values.
Results may differ from a plain program's by a relative error of at most 0.0079.
Values may be sent and summed in bfloat16 or wider, within the bound.
A program may use at most 128 MiB of HBM per device.

v0:
```python
import jax
import jax.numpy as jnp
from jax import lax
from jax.sharding import PartitionSpec as P

F = 256
HID = 256
CLS = 64
B = 256
PR = 2
STEP = 7
PROWS = 834
PIECES = 417
learn_rate = 0.01
beta_one = 0.5
beta_two = 0.5
adam_epsilon = 1e-08
decay_rate = 0.1


def contract_rows(left, right):
    return lax.dot_general(
        left, right, (((0,), (0,)), ((), ())), preferred_element_type=jnp.float32
    )


def contract_cols(left, right):
    return lax.dot_general(
        left, right, (((1,), (1,)), ((), ())), preferred_element_type=jnp.float32
    )


def body(
    features,
    adj_tiles,
    block_pairs,
    tile_count,
    degree,
    labels,
    loss_mask,
    slot_piece,
    master,
    moment_one,
    moment_two,
):
    col_count = lax.axis_size("col")
    grp_count = lax.axis_size("grp")
    col_index = lax.axis_index("col")
    grp_index = lax.axis_index("grp")
    node_rows = features.shape[0]
    group_nodes = degree.shape[0]
    block_count = group_nodes // B
    tile_slots = adj_tiles.shape[0]
    slot_width = slot_piece.shape[1]
    col_width = master.shape[2]
    own_slots = master.astype(jnp.bfloat16)[None]
    gathered = lax.all_gather(own_slots, ("grp", "col"), axis=0, tiled=True)
    slot_values = gathered.reshape(grp_count, col_count, slot_width, PR, col_width)
    slot_values = slot_values.transpose(0, 2, 3, 1, 4).reshape(
        grp_count * slot_width, PR, col_count * col_width
    )
    flat_slots = slot_piece.reshape(-1)
    positions = jnp.arange(flat_slots.shape[0], dtype=jnp.int32)
    target = jnp.where(flat_slots >= 0, flat_slots, PIECES)
    piece_slot = jnp.zeros((PIECES + 1,), jnp.int32).at[target].set(positions)[:PIECES]
    weight_table = slot_values[piece_slot].reshape(PROWS, HID)
    encoder_weight = weight_table[:F]
    self_weight = weight_table[F : F + HID]
    neigh_weight = weight_table[F + HID : F + 2 * HID]
    head_weight = weight_table[F + 2 * HID : F + 2 * HID + CLS]
    encoder_bias = weight_table[PROWS - 2].astype(jnp.float32)
    sage_bias = weight_table[PROWS - 1].astype(jnp.float32)
    mask_values = loss_mask.astype(jnp.float32)
    labelled = lax.psum(jnp.sum(mask_values), ("grp", "col"))
    preact = jnp.dot(features, encoder_weight, preferred_element_type=jnp.float32) + encoder_bias
    sig_pre = jax.nn.sigmoid(preact)
    encoded = (preact * sig_pre).astype(jnp.bfloat16)
    enc_columns = lax.all_to_all(encoded, "col", split_axis=1, concat_axis=0, tiled=True)
    pairs = block_pairs[0]
    row_blocks = pairs[:, 0]
    col_blocks = pairs[:, 1]
    live_tiles = jnp.arange(tile_slots, dtype=jnp.int32) < tile_count[0]
    block_ids = jnp.arange(block_count, dtype=jnp.int32)
    row_places = ((row_blocks[None, :] == block_ids[:, None]) & live_tiles[None, :]).astype(
        jnp.float32
    )
    picked = enc_columns.reshape(block_count, B, -1)[col_blocks]
    products = jnp.einsum("tij,tjc->tic", adj_tiles, picked, preferred_element_type=jnp.float32)
    block_sums = jnp.einsum("rt,tic->ric", row_places, products, precision=lax.Precision.HIGHEST)
    degree_values = degree.astype(jnp.float32)
    mean_columns = (block_sums.reshape(group_nodes, -1) / degree_values[:, None]).astype(
        jnp.bfloat16
    )
    neigh_mean = lax.all_to_all(mean_columns, "col", split_axis=0, concat_axis=1, tiled=True)
    sage_pre = (
        jnp.dot(encoded, self_weight, preferred_element_type=jnp.float32)
        + jnp.dot(neigh_mean, neigh_weight, preferred_element_type=jnp.float32)
        + sage_bias
    )
    sig_sage = jax.nn.sigmoid(sage_pre)
    hidden = (sage_pre * sig_sage).astype(jnp.bfloat16)
    logits = contract_cols(hidden, head_weight)
    row_max = jnp.max(logits, axis=1, keepdims=True)
    log_total = row_max[:, 0] + jnp.log(jnp.sum(jnp.exp(logits - row_max), axis=1))
    label_hot = (labels[:, None] == jnp.arange(CLS, dtype=jnp.int32)[None, :]).astype(jnp.float32)
    target_logit = jnp.sum(logits * label_hot, axis=1)
    local_loss = jnp.sum(mask_values * (log_total - target_logit))
    probability = jnp.exp(logits - log_total[:, None])
    logit_grad = ((probability - label_hot) * mask_values[:, None] / labelled).astype(jnp.bfloat16)
    head_grad = contract_rows(logit_grad, hidden)
    hidden_grad = jnp.dot(logit_grad, head_weight, preferred_element_type=jnp.float32)
    sage_grad = (hidden_grad * sig_sage * (1.0 + sage_pre * (1.0 - sig_sage))).astype(jnp.bfloat16)
    self_grad = contract_rows(encoded, sage_grad)
    neigh_grad = contract_rows(neigh_mean, sage_grad)
    sage_bias_grad = jnp.sum(sage_grad.astype(jnp.float32), axis=0)
    self_back = contract_cols(sage_grad, self_weight)
    neigh_back = contract_cols(sage_grad, neigh_weight)
    degree_rows = lax.dynamic_slice_in_dim(degree_values, col_index * node_rows, node_rows)
    sum_grad = (neigh_back / degree_rows[:, None]).astype(jnp.bfloat16)
    grad_columns = lax.all_to_all(sum_grad, "col", split_axis=1, concat_axis=0, tiled=True)
    picked_grad = grad_columns.reshape(block_count, B, -1)[row_blocks]
    back_products = jnp.einsum(
        "tij,tic->tjc", adj_tiles, picked_grad, preferred_element_type=jnp.float32
    )
    col_places = ((col_blocks[None, :] == block_ids[:, None]) & live_tiles[None, :]).astype(
        jnp.float32
    )
    back_blocks = jnp.einsum(
        "rt,tjc->rjc", col_places, back_products, precision=lax.Precision.HIGHEST
    )
    neigh_return = lax.all_to_all(
        back_blocks.reshape(group_nodes, -1).astype(jnp.bfloat16),
        "col",
        split_axis=0,
        concat_axis=1,
        tiled=True,
    ).astype(jnp.float32)
    encoded_grad = self_back + neigh_return
    preact_grad = (encoded_grad * sig_pre * (1.0 + preact * (1.0 - sig_pre))).astype(jnp.bfloat16)
    encoder_grad = contract_rows(features, preact_grad)
    encoder_bias_grad = jnp.sum(preact_grad.astype(jnp.float32), axis=0)
    grad_table = jnp.concatenate(
        [
            encoder_grad,
            self_grad,
            neigh_grad,
            head_grad,
            encoder_bias_grad[None, :],
            sage_bias_grad[None, :],
        ],
        axis=0,
    )
    loss_total = lax.psum(local_loss, ("grp", "col"))
    mean_loss = loss_total / labelled
    group_grad = lax.psum_scatter(
        grad_table.astype(jnp.bfloat16), "col", scatter_dimension=1, tiled=True
    ).astype(jnp.float32)
    my_pieces = lax.dynamic_slice_in_dim(slot_piece, grp_index, 1, 0)[0]
    is_owned = my_pieces >= 0
    safe_pieces = jnp.where(is_owned, my_pieces, 0)
    owned_values = is_owned[:, None, None]
    total_grad = lax.psum(group_grad, "grp")
    slot_grad = jnp.where(owned_values, total_grad.reshape(PIECES, PR, -1)[safe_pieces], 0.0)
    table_rows = safe_pieces[:, None] * PR + jnp.arange(PR, dtype=jnp.int32)[None, :]
    decay_values = jnp.where(table_rows < PROWS - 2, decay_rate, 0.0)[:, :, None]
    first_moment = beta_one * moment_one + (1.0 - beta_one) * slot_grad
    second_moment = beta_two * moment_two + (1.0 - beta_two) * slot_grad * slot_grad
    first_hat = first_moment / (1.0 - beta_one**STEP)
    second_hat = second_moment / (1.0 - beta_two**STEP)
    updated = master - learn_rate * (
        first_hat / (jnp.sqrt(second_hat) + adam_epsilon) + decay_values * master
    )
    updated = jnp.where(owned_values, updated, 0.0)
    first_moment = jnp.where(owned_values, first_moment, 0.0)
    second_moment = jnp.where(owned_values, second_moment, 0.0)
    return (mean_loss, updated, first_moment, second_moment, updated.astype(jnp.bfloat16))


def solution(mesh):
    in_specs = (
        P(("grp", "col"), None),
        P("grp", None, None),
        P("grp", None, None),
        P("grp"),
        P("grp"),
        P(("grp", "col")),
        P(("grp", "col")),
        P(),
        P("grp", None, "col"),
        P("grp", None, "col"),
        P("grp", None, "col"),
    )
    out_specs = (
        P(),
        P("grp", None, "col"),
        P("grp", None, "col"),
        P("grp", None, "col"),
        P("grp", None, "col"),
    )
    return jax.shard_map(body, mesh=mesh, in_specs=in_specs, out_specs=out_specs, check_vma=False)
```

profile of v0, /device:TPU:0, one launch (start us, length us, event | category | flops | bytes accessed | tf_op | source)
XLA Modules:
  0.0 409.3 jit_solution(9063719519104682953)
XLA Ops:
  7.2 0.9 convert_element_type.70
  8.2 46.8 %all-gather = bf16[2528,2,64]{2,1,0:T(2,128)(2,1)S(1)} all-gather(bf16[79,2,64]{2,1,0:T(2,128)(2,1)S(1)} %copy.83), channel_id=2, replica_groups=mesh['grp'=8,'col'=4] {'grp','col'}, dimensions={0}, use_global_device_ids=true | all-gather | bytes 667392 | tf_op jit(solution)/shard_map/all_gather | solution.py:57
  55.0 1.1 copy.84
  56.1 0.8 reshape.171
  57.0 1.2 copy.85
  58.3 4.1 scatter_custom_fusion
  62.4 2.7 gather_fusion
  66.7 2.5 multiply_convert_fusion.1
  69.2 3.9 all-to-all-start
  73.9 13.6 %all-to-all-done = bf16[2048,4,64]{0,2,1:T(8,128)(2,1)S(1)} async-done(((bf16[2048,4,64]{0,2,1:T(8,128)(2,1)}), bf16[2048,4,64]{0,2,1:T(8,128)(2,1)S(1)}, u32[]{:S(2)}, u32[]{:S(2)}) %all-to-all-start) | async-done | bytes 1048608 | tf_op jit(solution)/shard_map/all_to_all | solution.py:78
  87.6 0.8 copy.86
  88.4 1.6 reshape.174
  89.9 1.8 copy.87
  91.8 8.0 %gather_fusion.1 = bf16[192,256,64]{1,2,0:T(8,128)(2,1)} fusion(bf16[32,256,64]{1,2,0:T(8,128)(2,1)S(1)} %copy.87, s32[1024]{0:T(1024)S(1)} %pad_clamp_fusion.2), kind=kCustom, calls=%fused_computation.1 | custom fusion | bytes 12583680 | tf_op jit(solution)/shard_map/gather | solution.py:87
  99.7 18.3 %convolution_bitcast_fusion.1 = f32[192,256,64]{1,2,0:T(8,128)} fusion(bf16[192,256,64]{1,2,0:T(8,128)(2,1)} %gather_fusion.1, bf16[192,256,256]{2,1,0:T(8,128)(2,1)} %param.12), kind=kOutput, calls=%fused_computation.10 | convolution fusion | flops 1610612736 | bytes 44040192 | tf_op jit(solution)/shard_map/tij,tjc->tic/dot_general | solution.py:88
  118.1 16.9 %fusion.2 = f32[32,256,64]{1,0,2:T(8,128)} fusion(f32[192,256,64]{1,2,0:T(8,128)} %convolution_bitcast_fusion.1, s32[192]{0:T(256)S(1)} %bitcast.95, pred[192]{0:T(512)(128)(4,1)S(1)} %iota_compare_fusion.3), kind=kOutput, calls=%fused_computation.7 | convolution fusion | flops 1207971840 | bytes 14681024 | tf_op jit(solution)/shard_map/rt,tic->ric/dot_general | solution.py:89
  134.9 2.2 reshape.175
  137.1 2.1 fusion.12
  139.3 3.6 all-to-all-start.1
  143.1 3.0 fusion.40
  146.2 11.1 %all-to-all-done.1 = bf16[4,2048,64]{1,2,0:T(8,128)(2,1)S(1)} async-done(((bf16[4,2048,64]{1,2,0:T(8,128)(2,1)}), bf16[4,2048,64]{1,2,0:T(8,128)(2,1)S(1)}, u32[]{:S(2)}, u32[]{:S(2)}) %all-to-all-start.1) | async-done | bytes 1048608 | tf_op jit(solution)/shard_map/all_to_all | solution.py:94
  157.3 3.7 multiply_convert_fusion
  161.0 1.0 copy-done.6
  163.1 37.2 %all-reduce = (f32[]{:T(128)}, f32[]{:T(128)}) all-reduce(f32[]{:T(128)} %get-tuple-element.27, f32[]{:T(128)} %get-tuple-element.28), channel_id=1, replica_groups=mesh['grp'=8,'col'=4] {'grp','col'}, use_global_device_ids=true, to_apply=%region_7.8 | all-reduce | flops 2 | bytes 16 | tf_op jit(solution)/shard_map/psum | solution.py:74
  200.4 3.4 fusion.39
  203.8 1.4 fusion.10
  205.2 3.5 all-to-all-start.2
  208.8 14.4 %all-to-all-done.2 = bf16[2048,4,64]{0,2,1:T(8,128)(2,1)S(1)} async-done(((bf16[2048,4,64]{0,2,1:T(8,128)(2,1)}), bf16[2048,4,64]{0,2,1:T(8,128)(2,1)S(1)}, u32[]{:S(2)}, u32[]{:S(2)}) %all-to-all-start.2) | async-done | bytes 1048608 | tf_op jit(solution)/shard_map/all_to_all | solution.py:120
  223.2 1.8 copy.94
  225.0 2.6 reshape.176
  227.6 1.8 copy.95
  229.4 8.0 %gather_fusion.2 = bf16[192,256,64]{1,2,0:T(8,128)(2,1)} fusion(bf16[32,256,64]{1,2,0:T(8,128)(2,1)S(1)} %copy.95, s32[1024]{0:T(1024)S(1)} %pad_clamp_fusion.1), kind=kCustom, calls=%fused_computation.2 | custom fusion | bytes 12583680 | tf_op jit(solution)/shard_map/gather | solution.py:121
  237.3 19.0 %convolution_bitcast_fusion = f32[192,256,64]{1,2,0:T(8,128)} fusion(bf16[192,256,64]{1,2,0:T(8,128)(2,1)} %gather_fusion.2, bf16[192,256,256]{2,1,0:T(8,128)(2,1)} %param.12), kind=kOutput, calls=%fused_computation.9 | convolution fusion | flops 1610612736 | bytes 44040192 | tf_op jit(solution)/shard_map/tij,tic->tjc/dot_general | solution.py:122
  256.3 16.4 %fusion.13 = bf16[32,256,64]{1,0,2:T(8,128)(2,1)} fusion(f32[192,256,64]{1,2,0:T(8,128)} %convolution_bitcast_fusion, s32[192]{0:T(256)S(1)} %bitcast.94, pred[192]{0:T(512)(128)(4,1)S(1)} %iota_compare_fusion.3), kind=kOutput, calls=%fused_computation.30 | convolution fusion | flops 1208496128 | bytes 13632448 | tf_op jit(solution)/shard_map/rt,tjc->rjc/dot_general | solution.py:128
  272.8 1.9 convert_element_type.80
  274.6 1.6 copy.97
  276.2 3.5 all-to-all-start.3
  279.8 3.2 convolution_convert_fusion.3
  283.4 1.7 convolution_convert_fusion.1
  285.1 9.0 %all-to-all-done.3 = bf16[4,2048,64]{1,2,0:T(8,128)(2,1)S(1)} async-done(((bf16[4,2048,64]{1,2,0:T(8,128)(2,1)}), bf16[4,2048,64]{1,2,0:T(8,128)(2,1)S(1)}, u32[]{:S(2)}, u32[]{:S(2)}) %all-to-all-start.3) | async-done | bytes 1048608 | tf_op jit(solution)/shard_map/all_to_all | solution.py:131
  294.4 1.3 copy-done.18
  295.7 1.2 fusion.38
  297.7 1.0 copy.110
  299.1 21.4 %reduce-scatter.4.cloned.1.call-done = bf16[64,834]{1,0:T(8,128)(2,1)} async-done(((bf16[256,834]{1,0:T(8,128)(2,1)}), bf16[64,834]{1,0:T(8,128)(2,1)}) %reduce-scatter.4.cloned.1.call-update) | async-done | bytes 106768
  320.6 1.1 copy.111
  321.7 1.0 reshape.177
  324.1 71.9 %all-reduce.3.cloned.1.call-done = f32[417,2,64]{2,1,0:T(2,128)} async-done(((f32[417,2,64]{2,1,0:T(2,128)}), f32[417,2,64]{2,1,0:T(2,128)}) %all-reduce.3.cloned.1.call-update) | async-done | bytes 213520 | tf_op jit(solution)/shard_map/psum | solution.py:162
  396.1 1.7 gather_fusion.3
  (86 shorter events, 8.5 us)
Async XLA Ops:
  7.2 59.5 %copy-start = (bf16[2048,256]{1,0:T(8,128)(2,1)S(1)}, bf16[2048,256]{1,0:T(8,128)(2,1)}, u32[]{:S(2)}) copy-start(bf16[2048,256]{1,0:T(8,128)(2,1)} %param.11) | copy-start | bytes 3145732
  55.0 3.2 copy-start.15
  65.1 4.1 %copy-start.4 = (bf16[417,2,256]{2,1,0:T(2,128)(2,1)}, bf16[417,2,256]{2,1,0:T(2,128)(2,1)S(1)}, u32[]{:S(2)}) copy-start(bf16[417,2,256]{2,1,0:T(2,128)(2,1)S(1)} %gather_fusion) | copy-start | bytes 1281028
  69.2 4.6 %copy-start.11 = (s32[8192]{0:T(1024)S(1)}, s32[8192]{0:T(1024)}, u32[]{:S(2)}) copy-start(s32[8192]{0:T(1024)} %param.15) | copy-start | bytes 98308
  69.2 4.7 %copy-start.16 = (s32[1,192,2]{1,2,0:T(2,128)S(1)}, s32[1,192,2]{1,2,0:T(2,128)}, u32[]{:S(2)}) copy-start(s32[1,192,2]{1,2,0:T(2,128)} %param.13) | copy-start | bytes 4612
  69.2 18.3 %all-to-all-start = ((bf16[2048,4,64]{0,2,1:T(8,128)(2,1)}), bf16[2048,4,64]{0,2,1:T(8,128)(2,1)S(1)}, u32[]{:S(2)}, u32[]{:S(2)}) async-start(bf16[2048,4,64]{0,2,1:T(8,128)(2,1)} %bitcast.8), calls=%async_computation | async-start | bytes 2097152 | tf_op jit(solution)/shard_map/all_to_all | solution.py:78
  73.9 13.7 %copy-start.8 = (f32[8192]{0:T(1024)}, f32[8192]{0:T(1024)S(1)}, u32[]{:S(2)}) copy-start(f32[8192]{0:T(1024)S(1)} %convert_element_type.72) | copy-start | bytes 98308
  139.2 3.8 slice-start
  139.2 3.8 copy-start.12
  139.3 18.1 %all-to-all-start.1 = ((bf16[4,2048,64]{1,2,0:T(8,128)(2,1)}), bf16[4,2048,64]{1,2,0:T(8,128)(2,1)S(1)}, u32[]{:S(2)}, u32[]{:S(2)}) async-start(bf16[4,2048,64]{1,2,0:T(8,128)(2,1)} %fusion.12), calls=%async_computation.1 | async-start | bytes 2097152 | tf_op jit(solution)/shard_map/all_to_all | solution.py:94
  142.9 14.4 %copy-start.17 = (f32[1,256]{1,0:T(1,128)S(1)}, f32[1,256]{1,0:T(1,128)}, u32[]{:S(2)}) copy-start(f32[1,256]{1,0:T(1,128)} %get-tuple-element.34) | copy-start | bytes 3076
  157.3 5.0 %copy-start.14 = (s32[2048]{0:T(1024)S(1)}, s32[2048]{0:T(1024)}, u32[]{:S(2)}) copy-start(s32[2048]{0:T(1024)} %param.16) | copy-start | bytes 24580
  161.0 1.0 copy-start.6
  162.3 41.4 %copy-start.5 = (f32[2048,64]{0,1:T(8,128)}, f32[2048,64]{0,1:T(8,128)S(1)}, u32[]{:S(2)}) copy-start(f32[2048,64]{0,1:T(8,128)S(1)} %get-tuple-element.50) | copy-start | bytes 1572868
  200.4 3.4 dynamic-slice-start
  203.8 1.5 copy-start.1
  205.2 18.0 %all-to-all-start.2 = ((bf16[2048,4,64]{0,2,1:T(8,128)(2,1)}), bf16[2048,4,64]{0,2,1:T(8,128)(2,1)S(1)}, u32[]{:S(2)}, u32[]{:S(2)}) async-start(bf16[2048,4,64]{0,2,1:T(8,128)(2,1)} %bitcast.92), calls=%async_computation.2 | async-start | bytes 2097152 | tf_op jit(solution)/shard_map/all_to_all | solution.py:120
  276.2 17.9 %all-to-all-start.3 = ((bf16[4,2048,64]{1,2,0:T(8,128)(2,1)}), bf16[4,2048,64]{1,2,0:T(8,128)(2,1)S(1)}, u32[]{:S(2)}, u32[]{:S(2)}) async-start(bf16[4,2048,64]{1,2,0:T(8,128)(2,1)} %copy.97), calls=%async_computation.3 | async-start | bytes 2097152 | tf_op jit(solution)/shard_map/all_to_all | solution.py:131
  279.7 40.9 %reduce-scatter.4.cloned.1.call-start = ((), (), s32[]{:S(2)}) async-start(), calls=%async_computation.6 | async-start | bytes 573440
  279.7 3.2 copy-start.2
  285.1 9.2 %copy-start.3 = (bf16[2048,256]{0,1:T(8,128)(2,1)S(1)}, bf16[2048,256]{0,1:T(8,128)(2,1)}, u32[]{:S(2)}) copy-start(bf16[2048,256]{0,1:T(8,128)(2,1)} %copy-done.1) | copy-start | bytes 3145732
  294.1 1.6 copy-start.18
  296.9 0.8 copy-start.13
  296.9 1.9 copy-start.7
  296.9 2.0 copy-start.9
  296.9 2.1 copy-start.10
  298.7 97.4 %all-reduce.3.cloned.1.call-start = ((), (), s32[]{:S(2)}) async-start(), calls=%async_computation.5 | async-start | bytes 854016 | tf_op jit(solution)/shard_map/psum | solution.py:162
Sparse Core Ops, SparseCore 0:
  298.8 21.7 reduce-scatter.3
  324.0 72.0 all-reduce.2
where the time goes:
time: 415 us; the launch traced here: 409 us
  waiting for transfers between devices  142 us (34%)
  matrix products  92.1 us (22%)
  blocking collectives  84 us (20%)
  local copies, waits for them, and re-layouts  53.8 us (13%)
  between operations  17.9 us (4%)
  starting transfers between devices  14.7 us (4%)
  other arithmetic  5.23 us (1%)
    psum x1, waiting for transfers between devices, body(): total_grad = lax.psum(group_grad, 'grp')  71.9 us
    all_gather x1, blocking collectives, body(): gathered = lax.all_gather(own_slots, ('grp', 'col'), axis=0, tiled=True)  46.8 us
    psum x1, blocking collectives, body(): labelled = lax.psum(jnp.sum(mask_values), ('grp', 'col'))  37.2 us
    unnamed x3, waiting for transfers between devices  21.5 us
    dot_general x1, matrix products, body(): jnp.einsum('tij,tic->tjc', adj_tiles, picked_grad, preferred_element_type...  19 us
    dot_general x1, matrix products, body(): jnp.einsum('tij,tjc->tic', adj_tiles, picked, preferred_element_type=jnp....  18.3 us
    dot_general x1, matrix products, body(): jnp.einsum('rt,tic->ric', row_places, products, precision=lax.Precision.H...  16.9 us
    dot_general x1, matrix products, body(): jnp.einsum('rt,tjc->rjc', col_places, back_products, precision=lax.Precis...  16.4 us
  transfers between devices with their start and end apart: 6, of which 6 were waited for; matrix products, arithmetic and copies ran while one was open for 2% of the time, Pallas kernels for 0%

commit v1 on v0

--- a/solution.py
+++ b/solution.py
@@ -159,7 +159,11 @@
     is_owned = my_pieces >= 0
     safe_pieces = jnp.where(is_owned, my_pieces, 0)
     owned_values = is_owned[:, None, None]
-    total_grad = lax.psum(group_grad, "grp")
+    total_grad = group_grad
+    for hop in (1, 2, 4):
+        total_grad = total_grad + lax.ppermute(
+            total_grad, "grp", [(dev, dev ^ hop) for dev in range(8)]
+        )
     slot_grad = jnp.where(owned_values, total_grad.reshape(PIECES, PR, -1)[safe_pieces], 0.0)
     table_rows = safe_pieces[:, None] * PR + jnp.arange(PR, dtype=jnp.int32)[None, :]
     decay_values = jnp.where(table_rows < PROWS - 2, decay_rate, 0.0)[:, :, None]

time: 415 us -> 383 us (0.923)
  waiting for transfers between devices: 142 us -> 105 us
  starting transfers between devices: 14.7 us -> 20.5 us
    psum x1 -> x0, waiting for transfers between devices: 71.9 us -> none  [body(): total_grad = lax.psum(group_grad, 'grp')]
    ppermute x0 -> x3, waiting for transfers between devices: none -> 35.2 us  [body(): lax.ppermute(total_grad, 'grp', [(dev, dev ^ hop) for dev in range(8)])]
    ppermute x0 -> x3, starting transfers between devices: none -> 5.54 us  [body(): lax.ppermute(total_grad, 'grp', [(dev, dev ^ hop) for dev in range(8)])]
    unnamed x3 -> x2, waiting for transfers between devices: 21.5 us -> 21.6 us
  transfers between devices with their start and end apart: 6 -> 8, of which waited for: 6 -> 8; matrix products, arithmetic and copies ran while one was open for 2% -> 2% of each run, Pallas kernels for 0% -> 0%
where the time goes in v1:
time: 383 us; the launch traced here: 377 us
  waiting for transfers between devices  105 us (27%)
  matrix products  92.2 us (24%)
  blocking collectives  84 us (22%)
  local copies, waits for them, and re-layouts  52 us (14%)
  starting transfers between devices  20.5 us (5%)
  between operations  17.9 us (5%)
  other arithmetic  5.4 us (1%)
    all_gather x1, blocking collectives, body(): gathered = lax.all_gather(own_slots, ('grp', 'col'), axis=0, tiled=True)  46.8 us
    psum x1, blocking collectives, body(): loss_total = lax.psum(local_loss, ('grp', 'col'))  37.2 us
    ppermute x3, waiting for transfers between devices, body(): lax.ppermute(total_grad, 'grp', [(dev, dev ^ hop) for dev in range(8)])  35.2 us
    unnamed x2, waiting for transfers between devices  21.6 us
    dot_general x1, matrix products, body(): jnp.einsum('tij,tic->tjc', adj_tiles, picked_grad, preferred_element_type...  19 us
    dot_general x1, matrix products, body(): jnp.einsum('tij,tjc->tic', adj_tiles, picked, preferred_element_type=jnp....  18.3 us
    dot_general x1, matrix products, body(): jnp.einsum('rt,tic->ric', row_places, products, precision=lax.Precision.H...  16.9 us
    dot_general x1, matrix products, body(): jnp.einsum('rt,tjc->rjc', col_places, back_products, precision=lax.Precis...  16.4 us
  transfers between devices with their start and end apart: 8, of which 8 were waited for; matrix products, arithmetic and copies ran while one was open for 2% of the time, Pallas kernels for 0%

profile of v1, /device:TPU:0, one launch (start us, length us, event | category | flops | bytes accessed | tf_op | source)
XLA Modules:
  0.0 376.8 jit_solution(17138335157911418881)
XLA Ops:
  8.2 46.8 %all-gather = bf16[2528,2,64]{2,1,0:T(2,128)(2,1)S(1)} all-gather(bf16[79,2,64]{2,1,0:T(2,128)(2,1)S(1)} %copy.83), channel_id=2, replica_groups=mesh['grp'=8,'col'=4] {'grp','col'}, dimensions={0}, use_global_device_ids=true | all-gather | bytes 667392 | tf_op jit(solution)/shard_map/all_gather | solution.py:57
  55.0 1.1 copy.84
  57.0 1.2 copy.85
  58.3 4.1 %scatter_custom_fusion = s32[418]{0:T(512)S(1)} fusion(s32[632]{0:T(1024)S(1)} %fusion.29, s32[632]{0:T(1024)S(1)} %iota.23, s32[]{:T(128)} %constant.21.clone.1), kind=kCustom, calls=%fused_computation.77 | custom fusion | bytes 1676 | tf_op jit(solution)/shard_map/scatter | solution.py:65
  62.4 2.7 gather_fusion
  66.7 2.5 multiply_convert_fusion.1
  69.2 4.0 %all-to-all-start = ((bf16[2048,4,64]{0,2,1:T(8,128)(2,1)}), bf16[2048,4,64]{0,2,1:T(8,128)(2,1)S(1)}, u32[]{:S(2)}, u32[]{:S(2)}) async-start(bf16[2048,4,64]{0,2,1:T(8,128)(2,1)} %bitcast.8), calls=%async_computation | async-start | bytes 2097152 | tf_op jit(solution)/shard_map/all_to_all | solution.py:78
  74.0 13.6 %all-to-all-done = bf16[2048,4,64]{0,2,1:T(8,128)(2,1)S(1)} async-done(((bf16[2048,4,64]{0,2,1:T(8,128)(2,1)}), bf16[2048,4,64]{0,2,1:T(8,128)(2,1)S(1)}, u32[]{:S(2)}, u32[]{:S(2)}) %all-to-all-start) | async-done | bytes 1048608 | tf_op jit(solution)/shard_map/all_to_all | solution.py:78
  88.4 1.6 reshape.174
  90.0 1.8 copy.87
  91.8 8.0 %gather_fusion.1 = bf16[192,256,64]{1,2,0:T(8,128)(2,1)} fusion(bf16[32,256,64]{1,2,0:T(8,128)(2,1)S(1)} %copy.87, s32[1024]{0:T(1024)S(1)} %pad_clamp_fusion.2), kind=kCustom, calls=%fused_computation.1 | custom fusion | bytes 12583680 | tf_op jit(solution)/shard_map/gather | solution.py:87
  99.8 18.3 %convolution_bitcast_fusion.1 = f32[192,256,64]{1,2,0:T(8,128)} fusion(bf16[192,256,64]{1,2,0:T(8,128)(2,1)} %gather_fusion.1, bf16[192,256,256]{2,1,0:T(8,128)(2,1)} %param.12), kind=kOutput, calls=%fused_computation.10 | convolution fusion | flops 1610612736 | bytes 44040192 | tf_op jit(solution)/shard_map/tij,tjc->tic/dot_general | solution.py:88
  118.1 16.9 %fusion.2 = f32[32,256,64]{1,0,2:T(8,128)} fusion(f32[192,256,64]{1,2,0:T(8,128)} %convolution_bitcast_fusion.1, s32[192]{0:T(256)S(1)} %bitcast.95, pred[192]{0:T(512)(128)(4,1)S(1)} %iota_compare_fusion.3), kind=kOutput, calls=%fused_computation.7 | convolution fusion | flops 1207971840 | bytes 14681024 | tf_op jit(solution)/shard_map/rt,tic->ric/dot_general | solution.py:89
  135.0 2.2 reshape.175
  137.3 2.1 fusion.12
  139.4 3.6 all-to-all-start.1
  143.2 3.1 fusion.40
  146.3 11.1 %all-to-all-done.1 = bf16[4,2048,64]{1,2,0:T(8,128)(2,1)S(1)} async-done(((bf16[4,2048,64]{1,2,0:T(8,128)(2,1)}), bf16[4,2048,64]{1,2,0:T(8,128)(2,1)S(1)}, u32[]{:S(2)}, u32[]{:S(2)}) %all-to-all-start.1) | async-done | bytes 1048608 | tf_op jit(solution)/shard_map/all_to_all | solution.py:94
  157.4 3.7 multiply_convert_fusion
  161.1 1.0 copy-done.6
  163.2 37.2 %all-reduce = (f32[]{:T(128)}, f32[]{:T(128)}) all-reduce(f32[]{:T(128)} %get-tuple-element.28, f32[]{:T(128)} %get-tuple-element.27), channel_id=1, replica_groups=mesh['grp'=8,'col'=4] {'grp','col'}, use_global_device_ids=true, to_apply=%region_5.6 | all-reduce | flops 2 | bytes 16 | tf_op jit(solution)/shard_map/psum | solution.py:153
  200.5 3.4 fusion.39
  203.9 1.4 fusion.10
  205.3 3.5 all-to-all-start.2
  208.9 14.4 %all-to-all-done.2 = bf16[2048,4,64]{0,2,1:T(8,128)(2,1)S(1)} async-done(((bf16[2048,4,64]{0,2,1:T(8,128)(2,1)}), bf16[2048,4,64]{0,2,1:T(8,128)(2,1)S(1)}, u32[]{:S(2)}, u32[]{:S(2)}) %all-to-all-start.2) | async-done | bytes 1048608 | tf_op jit(solution)/shard_map/all_to_all | solution.py:120
  223.3 1.8 copy.94
  225.1 2.6 reshape.176
  227.7 1.8 copy.95
  229.5 8.0 %gather_fusion.2 = bf16[192,256,64]{1,2,0:T(8,128)(2,1)} fusion(bf16[32,256,64]{1,2,0:T(8,128)(2,1)S(1)} %copy.95, s32[1024]{0:T(1024)S(1)} %pad_clamp_fusion.1), kind=kCustom, calls=%fused_computation.2 | custom fusion | bytes 12583680 | tf_op jit(solution)/shard_map/gather | solution.py:121
  237.5 19.0 %convolution_bitcast_fusion = f32[192,256,64]{1,2,0:T(8,128)} fusion(bf16[192,256,64]{1,2,0:T(8,128)(2,1)} %gather_fusion.2, bf16[192,256,256]{2,1,0:T(8,128)(2,1)} %param.12), kind=kOutput, calls=%fused_computation.9 | convolution fusion | flops 1610612736 | bytes 44040192 | tf_op jit(solution)/shard_map/tij,tic->tjc/dot_general | solution.py:122
  256.5 16.4 %fusion.13 = bf16[32,256,64]{1,0,2:T(8,128)(2,1)} fusion(f32[192,256,64]{1,2,0:T(8,128)} %convolution_bitcast_fusion, s32[192]{0:T(256)S(1)} %bitcast.94, pred[192]{0:T(512)(128)(4,1)S(1)} %iota_compare_fusion.3), kind=kOutput, calls=%fused_computation.30 | convolution fusion | flops 1208496128 | bytes 13632448 | tf_op jit(solution)/shard_map/rt,tjc->rjc/dot_general | solution.py:128
  272.9 1.9 convert_element_type.80
  274.8 1.6 copy.97
  276.3 3.5 all-to-all-start.3
  280.2 3.2 convolution_convert_fusion.3
  283.8 1.7 convolution_convert_fusion.1
  285.5 8.7 %all-to-all-done.3 = bf16[4,2048,64]{1,2,0:T(8,128)(2,1)S(1)} async-done(((bf16[4,2048,64]{1,2,0:T(8,128)(2,1)}), bf16[4,2048,64]{1,2,0:T(8,128)(2,1)S(1)}, u32[]{:S(2)}, u32[]{:S(2)}) %all-to-all-start.3) | async-done | bytes 1048608 | tf_op jit(solution)/shard_map/all_to_all | solution.py:131
  294.5 1.3 copy-done.18
  295.8 1.2 fusion.38
  297.8 1.0 copy.110
  299.2 21.6 %reduce-scatter.4.cloned.1.call-done = bf16[64,834]{1,0:T(8,128)(2,1)} async-done(((bf16[256,834]{1,0:T(8,128)(2,1)}), bf16[64,834]{1,0:T(8,128)(2,1)}) %reduce-scatter.4.cloned.1.call-update) | async-done | bytes 106768
  320.8 1.1 copy.111
  321.9 1.5 collective-permute-start
  323.4 10.0 %collective-permute-done = f32[834,64]{1,0:T(8,128)S(1)} collective-permute-done((f32[834,64]{1,0:T(8,128)S(1)}, f32[834,64]{1,0:T(8,128)S(1)}, u32[]{:S(2)}, u32[]{:S(2)}) %collective-permute-start) | collective-permute-done | bytes 213536 | tf_op jit(solution)/shard_map/ppermute | solution.py:164
  333.5 1.5 collective-permute-start.1
  335.0 9.1 %collective-permute-done.1 = f32[834,64]{1,0:T(8,128)S(1)} collective-permute-done((f32[834,64]{1,0:T(8,128)S(1)}, f32[834,64]{1,0:T(8,128)S(1)}, u32[]{:S(2)}, u32[]{:S(2)}) %collective-permute-start.1) | collective-permute-done | bytes 213536 | tf_op jit(solution)/shard_map/ppermute | solution.py:164
  344.2 2.5 collective-permute-start.2
  348.1 16.1 %collective-permute-done.2 = f32[834,64]{1,0:T(8,128)S(1)} collective-permute-done((f32[834,64]{1,0:T(8,128)S(1)}, f32[834,64]{1,0:T(8,128)S(1)}, u32[]{:S(2)}, u32[]{:S(2)}) %collective-permute-start.2) | collective-permute-done | bytes 213536 | tf_op jit(solution)/shard_map/ppermute | solution.py:164
  (93 shorter events, 12.3 us)
Async XLA Ops:
  7.2 59.5 %copy-start = (bf16[2048,256]{1,0:T(8,128)(2,1)S(1)}, bf16[2048,256]{1,0:T(8,128)(2,1)}, u32[]{:S(2)}) copy-start(bf16[2048,256]{1,0:T(8,128)(2,1)} %param.11) | copy-start | bytes 3145732
  55.0 3.2 copy-start.15
  65.1 4.1 %copy-start.4 = (bf16[417,2,256]{2,1,0:T(2,128)(2,1)}, bf16[417,2,256]{2,1,0:T(2,128)(2,1)S(1)}, u32[]{:S(2)}) copy-start(bf16[417,2,256]{2,1,0:T(2,128)(2,1)S(1)} %gather_fusion) | copy-start | bytes 1281028
  69.2 4.6 %copy-start.11 = (s32[8192]{0:T(1024)S(1)}, s32[8192]{0:T(1024)}, u32[]{:S(2)}) copy-start(s32[8192]{0:T(1024)} %param.15) | copy-start | bytes 98308
  69.2 4.7 %copy-start.16 = (s32[1,192,2]{1,2,0:T(2,128)S(1)}, s32[1,192,2]{1,2,0:T(2,128)}, u32[]{:S(2)}) copy-start(s32[1,192,2]{1,2,0:T(2,128)} %param.13) | copy-start | bytes 4612
  69.2 18.4 %all-to-all-start = ((bf16[2048,4,64]{0,2,1:T(8,128)(2,1)}), bf16[2048,4,64]{0,2,1:T(8,128)(2,1)S(1)}, u32[]{:S(2)}, u32[]{:S(2)}) async-start(bf16[2048,4,64]{0,2,1:T(8,128)(2,1)} %bitcast.8), calls=%async_computation | async-start | bytes 2097152 | tf_op jit(solution)/shard_map/all_to_all | solution.py:78
  73.9 13.7 %copy-start.8 = (f32[8192]{0:T(1024)}, f32[8192]{0:T(1024)S(1)}, u32[]{:S(2)}) copy-start(f32[8192]{0:T(1024)S(1)} %convert_element_type.72) | copy-start | bytes 98308
  139.4 3.8 %slice-start = ((bf16[417,2,256]{2,1,0:T(2,128)(2,1)}), bf16[32,2,256]{2,1,0:T(2,128)(2,1)S(1)}, s32[]{:S(2)}) async-start(bf16[417,2,256]{2,1,0:T(2,128)(2,1)} %copy-done.4), calls=%async_computation.6 | async-start | bytes 65536 | tf_op jit(solution)/shard_map/slice | solution.py:70
  139.4 3.8 %copy-start.12 = (s32[2048]{0:T(1024)S(1)}, s32[2048]{0:T(1024)}, u32[]{:S(2)}) copy-start(s32[2048]{0:T(1024)} %param.17) | copy-start | bytes 24580
  139.4 18.1 %all-to-all-start.1 = ((bf16[4,2048,64]{1,2,0:T(8,128)(2,1)}), bf16[4,2048,64]{1,2,0:T(8,128)(2,1)S(1)}, u32[]{:S(2)}, u32[]{:S(2)}) async-start(bf16[4,2048,64]{1,2,0:T(8,128)(2,1)} %fusion.12), calls=%async_computation.1 | async-start | bytes 2097152 | tf_op jit(solution)/shard_map/all_to_all | solution.py:94
  143.0 14.4 %copy-start.17 = (f32[1,256]{1,0:T(1,128)S(1)}, f32[1,256]{1,0:T(1,128)}, u32[]{:S(2)}) copy-start(f32[1,256]{1,0:T(1,128)} %get-tuple-element.34) | copy-start | bytes 3076
  157.4 5.0 %copy-start.14 = (s32[2048]{0:T(1024)S(1)}, s32[2048]{0:T(1024)}, u32[]{:S(2)}) copy-start(s32[2048]{0:T(1024)} %param.16) | copy-start | bytes 24580
  161.1 1.0 copy-start.6
  162.4 41.4 %copy-start.5 = (f32[2048,64]{0,1:T(8,128)}, f32[2048,64]{0,1:T(8,128)S(1)}, u32[]{:S(2)}) copy-start(f32[2048,64]{0,1:T(8,128)S(1)} %get-tuple-element.50) | copy-start | bytes 1572868
  200.5 3.4 dynamic-slice-start
  203.9 1.5 copy-start.1
  205.3 18.0 %all-to-all-start.2 = ((bf16[2048,4,64]{0,2,1:T(8,128)(2,1)}), bf16[2048,4,64]{0,2,1:T(8,128)(2,1)S(1)}, u32[]{:S(2)}, u32[]{:S(2)}) async-start(bf16[2048,4,64]{0,2,1:T(8,128)(2,1)} %bitcast.92), calls=%async_computation.2 | async-start | bytes 2097152 | tf_op jit(solution)/shard_map/all_to_all | solution.py:120
  276.3 17.9 %all-to-all-start.3 = ((bf16[4,2048,64]{1,2,0:T(8,128)(2,1)}), bf16[4,2048,64]{1,2,0:T(8,128)(2,1)S(1)}, u32[]{:S(2)}, u32[]{:S(2)}) async-start(bf16[4,2048,64]{1,2,0:T(8,128)(2,1)} %copy.97), calls=%async_computation.3 | async-start | bytes 2097152 | tf_op jit(solution)/shard_map/all_to_all | solution.py:131
  279.8 40.9 %reduce-scatter.4.cloned.1.call-start = ((), (), s32[]{:S(2)}) async-start(), calls=%async_computation.5 | async-start | bytes 573440
  280.1 3.2 copy-start.2
  285.5 9.0 %copy-start.3 = (bf16[2048,256]{0,1:T(8,128)(2,1)S(1)}, bf16[2048,256]{0,1:T(8,128)(2,1)}, u32[]{:S(2)}) copy-start(bf16[2048,256]{0,1:T(8,128)(2,1)} %copy-done.1) | copy-start | bytes 3145732
  294.2 1.6 copy-start.18
  297.0 0.8 copy-start.13
  297.0 1.8 copy-start.7
  297.0 1.9 copy-start.9
  297.0 2.0 copy-start.10
  321.9 11.6 %collective-permute-start = (f32[834,64]{1,0:T(8,128)S(1)}, f32[834,64]{1,0:T(8,128)S(1)}, u32[]{:S(2)}, u32[]{:S(2)}) collective-permute-start(f32[834,64]{1,0:T(8,128)S(1)} %convert_element_type.87), channel_id=1, source_target_pairs={{0,4},{4,0},{8,12},{12,8},{16,20},{20,16},{24,28},{28,24},{1,5},{5... | collective-permute-start | bytes 640520 | tf_op jit(solution)/shard_map/ppermute | solution.py:164
  333.5 10.7 %collective-permute-start.1 = (f32[834,64]{1,0:T(8,128)S(1)}, f32[834,64]{1,0:T(8,128)S(1)}, u32[]{:S(2)}, u32[]{:S(2)}) collective-permute-start(f32[834,64]{1,0:T(8,128)S(1)} %convert_add_fusion), channel_id=1, source_target_pairs={{0,8},{4,12},{8,0},{12,4},{16,24},{20,28},{24,16},{28,20},{1,9},{5... | collective-permute-start | bytes 640520 | tf_op jit(solution)/shard_map/ppermute | solution.py:164
  344.2 20.0 %collective-permute-start.2 = (f32[834,64]{1,0:T(8,128)S(1)}, f32[834,64]{1,0:T(8,128)S(1)}, u32[]{:S(2)}, u32[]{:S(2)}) collective-permute-start(f32[834,64]{1,0:T(8,128)S(1)} %add.172), channel_id=1, source_target_pairs={{0,16},{4,20},{8,24},{12,28},{16,0},{20,4},{24,8},{28,12},{1,17},{... | collective-permute-start | bytes 640520 | tf_op jit(solution)/shard_map/ppermute | solution.py:164
Sparse Core Ops, SparseCore 0:
  298.9 21.7 reduce-scatter.3
